TPU v7x, 32 devices: a whole 2x2x4 slice. The times are simulated.
32 devices in a mesh: groups: 2 (over x), rows: 4 (over y, core), cols: 4 (over z).
Axes of the slice: x: 2, y: 2, z: 4, core: 2. Of those that a mesh axis runs over, the one named last changes fastest.
Arguments:
- pair_state: float32 [768, 384, 128], P(('groups', 'rows'), 'cols'), parts along dimension 0, may hold values from -6 to 6
- token_mask: int32 [768], P('groups'), parts along dimension 0, may hold values 0 or 1
- norm_gain: float32 [2, 128], replicated, may hold values from 0.25 to 1.75
- norm_bias: float32 [2, 128], replicated, may hold values from -3 to 3
- proj_weight: float32 [2, 128, 512], replicated, may hold values from -0.5 to 0.5
- gate_weight: float32 [2, 128, 128], replicated, may hold values from -0.5 to 0.5
- out_gain: float32 [2, 128], replicated, may hold values from 0.25 to 1.75
- out_bias: float32 [2, 128], replicated, may hold values from -3 to 3
- out_weight: float32 [2, 128, 128], replicated, may hold values from -0.5 to 0.5
Outputs:
- pair_out: float32 [768, 384, 128], P(('groups', 'rows'), 'cols'), parts along dimension 0
There are 2 independent parts, one for each index of `groups`. A program takes and returns all parts, laid end to end along the dimension named above; an argument that names none is the same for every part. Nothing has to cross between parts.
All inputs are finite; a program needn't handle non-finite values.
Results may differ from a plain program's by a relative error of at most 0.0001.
Values sent between devices are 32-bit elements; how exact they have to be, the bound alone decides.
A program may use at most 128 MiB of HBM per device.

v0:
```python
import functools

import jax
import jax.numpy as jnp
from jax import lax
from jax.experimental import pallas as pl
from jax.experimental.pallas import tpu as pltpu
from jax.sharding import PartitionSpec as P

eps = 1e-05
precise = lax.Precision.HIGH
MESH = pl.DeviceIdType.MESH
LANES = 128
VMEM_LIMIT = 67_000_000


def normalize(values, gain, shift):
    center = values - jnp.mean(values, axis=-1, keepdims=True)
    spread = jnp.mean(center * center, axis=-1, keepdims=True)
    return center * lax.rsqrt(spread + eps) * gain + shift


def project(state, pair_mask, segment, norm_gain, norm_bias, proj_weight, gate_weight):
    width = proj_weight.shape[2] // 4
    normed = normalize(state, norm_gain[segment], norm_bias[segment])
    hidden = jnp.einsum(
        "ijc,cf->ijf", normed, proj_weight[segment], precision=precise
    )
    left_side = (
        pair_mask[:, :, None]
        * jax.nn.sigmoid(hidden[:, :, :width])
        * hidden[:, :, width : 2 * width]
    )
    right_side = (
        pair_mask[:, :, None]
        * jax.nn.sigmoid(hidden[:, :, 2 * width : 3 * width])
        * hidden[:, :, 3 * width :]
    )
    gating = jax.nn.sigmoid(
        jnp.einsum("ijc,cd->ijd", normed, gate_weight[segment], precision=precise)
    )
    return (left_side, right_side, gating)


def finish(state, mixed, gating, segment, out_gain, out_bias, out_weight):
    result = jnp.einsum(
        "ijh,hc->ijc",
        normalize(mixed, out_gain[segment], out_bias[segment]),
        out_weight[segment],
        precision=precise,
    )
    return state + gating * result


def plain_body(
    pair_state,
    token_mask,
    norm_gain,
    norm_bias,
    proj_weight,
    gate_weight,
    out_gain,
    out_bias,
    out_weight,
):
    row_count = pair_state.shape[0]
    col_count = pair_state.shape[1]
    row_start = lax.axis_index("rows") * row_count
    col_start = lax.axis_index("cols") * col_count
    maskf = token_mask.astype(jnp.float32)
    row_mask = lax.dynamic_slice_in_dim(maskf, row_start, row_count)
    col_mask = lax.dynamic_slice_in_dim(maskf, col_start, col_count)
    pair_mask = row_mask[:, None] * col_mask[None, :]
    left_side, right_side, gating = project(
        pair_state, pair_mask, 0, norm_gain, norm_bias, proj_weight, gate_weight
    )
    partial_out = jnp.einsum(
        "ikh,jkh->ijh",
        left_side,
        lax.all_gather(right_side, "rows", axis=0, tiled=True),
        precision=precise,
    )
    mixed = lax.psum_scatter(partial_out, "cols", scatter_dimension=1, tiled=True)
    updated = finish(pair_state, mixed, gating, 0, out_gain, out_bias, out_weight)
    left_next, right_next, gate_next = project(
        updated, pair_mask, 1, norm_gain, norm_bias, proj_weight, gate_weight
    )
    partial_in = jnp.einsum(
        "kih,kjh->ijh",
        lax.all_gather(left_next, "cols", axis=1, tiled=True),
        right_next,
        precision=precise,
    )
    mixed_next = lax.psum_scatter(partial_in, "rows", scatter_dimension=0, tiled=True)
    return finish(updated, mixed_next, gate_next, 1, out_gain, out_bias, out_weight)


def halves(x):
    high = x.astype(jnp.bfloat16)
    return high, (x - high.astype(jnp.float32)).astype(jnp.bfloat16)


def streamed(x):
    high, low = halves(x)
    return jnp.concatenate([high, low, high], axis=1)


def held(x):
    high, low = halves(x)
    return jnp.concatenate([high, high, low], axis=1)


def stacked(weight):
    rounded = lax.reduce_precision(weight, 8, 7)
    high, low = rounded.astype(jnp.bfloat16), (weight - rounded).astype(jnp.bfloat16)
    return jnp.concatenate([high, high, low], axis=0)


def times(x, weight3):
    return jnp.dot(streamed(x), weight3, preferred_element_type=jnp.float32)


def against(a3, b3):
    return lax.dot_general(
        a3, b3, (((1,), (1,)), ((), ())), preferred_element_type=jnp.float32
    )


def gated_three(normed, mask, weight3):
    hidden = times(normed, weight3)
    part = lambda f: hidden[:, f * LANES : (f + 1) * LANES]
    return (
        mask * jax.nn.sigmoid(part(0)) * part(1),
        mask * jax.nn.sigmoid(part(2)) * part(3),
        jax.nn.sigmoid(part(4)),
    )


def padded(x):
    rows = x.shape[0]
    if rows == LANES:
        return x
    return jnp.concatenate([x, jnp.zeros((LANES - rows, x.shape[1]), x.dtype)], axis=0)


def first_kernel(group, state, rmask, cmask, vec, weight3, left_t, right_t, gate):
    m, extent, _ = state.shape
    count = group * extent

    @pl.loop(0, m // group)
    def _(g):
        x = state[pl.ds(g * group, group)].reshape(count, LANES)
        normed = normalize(x, vec[0:1, :], vec[1:2, :])
        mask = (rmask[pl.ds(g * group, group)] * cmask[...][None]).reshape(count, LANES)
        left, right, gating = gated_three(normed, mask, weight3[...])
        gate[pl.ds(g * group, group)] = gating.reshape(group, extent, LANES)
        for b in range(group):
            rows = slice(b * extent, (b + 1) * extent)
            left_t[0, pl.ds(g * group + b, LANES, m), :] = padded(left[rows]).T
            right_t[0, pl.ds(g * group + b, LANES, m), :] = padded(right[rows]).T


def first_call(n, state, rmask, cmask, vec, weight3):
    extent = state.shape[0]
    m = extent // n
    turned = jax.ShapeDtypeStruct((n, LANES * m, LANES), jnp.float32)
    whole = lambda a: pl.BlockSpec(a.shape, lambda p: (0,) * a.ndim)
    return pl.pallas_call(
        functools.partial(first_kernel, 4),
        grid=(n,),
        in_specs=[
            pl.BlockSpec((m, extent, LANES), lambda p: (p, 0, 0)),
            pl.BlockSpec((m, 1, LANES), lambda p: (p, 0, 0)),
            whole(cmask), whole(vec), whole(weight3),
        ],
        out_specs=[
            pl.BlockSpec((1, LANES * m, LANES), lambda p: (p, 0, 0)),
            pl.BlockSpec((1, LANES * m, LANES), lambda p: (p, 0, 0)),
            pl.BlockSpec((m, extent, LANES), lambda p: (p, 0, 0)),
        ],
        out_shape=[turned, turned, jax.ShapeDtypeStruct(state.shape, jnp.float32)],
        compiler_params=pltpu.CompilerParams(vmem_limit_bytes=VMEM_LIMIT),
    )(state, rmask, cmask, vec, weight3)


def middle_kernel(
    rows, cols, n, parts,
    left_t, right_t, state, gate0, rmask, cmask, vec, out3, proj3,
    near, line, lefts, rights, state1, gate1,
    high, low, block, turned, chunk, from_left, from_right, tile, done,
    gather_send, gather_recv, load_sem, tile_sem,
    sum_send_r, sum_send_l, sum_recv_r, sum_recv_l,
    line_recv_r, line_recv_l, done_sem, forward_sem, spread_sem, left_recv, right_recv,
):
    m = tile.shape[2]
    extent = n * m
    ticks = n * parts
    last = cols - 1
    r, c = lax.axis_index("rows"), lax.axis_index("cols")
    back = last - c
    partner = r + 1 - 2 * lax.rem(r, 2)
    across = lax.rem(r + 2, rows)
    beyond = lax.rem(partner + 2, rows)

    barrier = pltpu.get_barrier_semaphore()
    for off in range(1, rows):
        pl.semaphore_signal(barrier, inc=1, device_id={"rows": lax.rem(r + off, rows)}, device_id_type=MESH)

    @pl.when(c > 0)
    def _():
        pl.semaphore_signal(barrier, inc=1, device_id={"cols": c - 1}, device_id_type=MESH)

    @pl.when(c < last)
    def _():
        pl.semaphore_signal(barrier, inc=1, device_id={"cols": c + 1}, device_id_type=MESH)

    pl.semaphore_wait(barrier, rows - 1 + jnp.minimum(c, 1) + jnp.minimum(back, 1))

    def remote(src, dst, send, recv, **where):
        return pltpu.make_async_remote_copy(
            src_ref=src, dst_ref=dst, send_sem=send, recv_sem=recv,
            device_id=where, device_id_type=MESH,
        )

    def to_partner(p):
        return remote(right_t.at[p], near.at[r, p], gather_send.at[0, p], gather_recv.at[0, p], rows=partner)

    def to_across(p):
        return remote(right_t.at[p], near.at[r, p], gather_send.at[1, p], gather_recv.at[1, p], rows=across)

    def relay(p):
        return remote(near.at[across, p], near.at[across, p], gather_send.at[2, p], gather_recv.at[2, p], rows=partner)

    def loads(p):
        return [
            pltpu.make_async_copy(right_t.at[p], block.at[r], load_sem.at[0]),
            pltpu.make_async_copy(near.at[partner, p], block.at[partner], load_sem.at[1]),
            pltpu.make_async_copy(near.at[across, p], block.at[across], load_sem.at[2]),
            pltpu.make_async_copy(near.at[beyond, p], block.at[beyond], load_sem.at[3]),
        ]

    for p in range(n):
        to_across(p).start()
        to_partner(p).start()

    fill = [
        pltpu.make_async_copy(left_t.at[p], turned.at[pl.ds(p * LANES * m, LANES * m)], load_sem.at[p])
        for p in range(n)
    ]
    for copy in fill:
        copy.start()
    for copy in fill:
        copy.wait()

    @pl.loop(0, LANES)
    def _(h):
        rows_of = [
            turned[pl.ds(pl.multiple_of(p * LANES * m + h * m, 8), m), :] for p in range(n)
        ]
        top, rest = halves(jnp.concatenate(rows_of, axis=0))
        high[h] = top
        low[h] = rest

    to_across(0).wait_recv()
    relay(0).start()
    to_partner(0).wait_recv()
    relay(0).wait_recv()
    for copy in loads(0):
        copy.start()

    def multiply():
        @pl.loop(0, LANES // 4)
        def _(g):
            for b in range(4):
                h = g * 4 + b
                at = pl.multiple_of(h * m, 8)
                right = padded(jnp.concatenate([block[o, pl.ds(at, m), :] for o in range(rows)], axis=0))
                a3 = jnp.concatenate([high[h], low[h], high[h]], axis=1)
                turned[pl.ds(h, extent, LANES), :] = against(a3, held(right))

    def turn(q, slot):
        @pl.loop(0, m)
        def _(i):
            at = pl.multiple_of((q * m + i) * LANES, LANES)
            straight = turned[pl.ds(at, LANES), :].T
            for d in range(cols):
                chunk[slot, d, i] = straight[d * m : (d + 1) * m]

    def sum_right(u, s):
        slot = lax.rem(u, 4)
        return remote(chunk.at[slot, c + last - s], from_left.at[u, s], sum_send_r.at[slot, s], sum_recv_r.at[u, s], cols=c + 1)

    def sum_left(u, s):
        slot = lax.rem(u, 4)
        return remote(chunk.at[slot, c - last + s], from_right.at[u, s], sum_send_l.at[slot, s], sum_recv_l.at[u, s], cols=c - 1)

    def arrived_right(u, s):
        return remote(chunk.at[0, 0], from_left.at[u, s], sum_send_r.at[0, s], sum_recv_r.at[u, s], cols=c - 1)

    def arrived_left(u, s):
        return remote(chunk.at[0, 0], from_right.at[u, s], sum_send_l.at[0, s], sum_recv_l.at[u, s], cols=c + 1)

    def add_to(slot, d, source, u, s):
        @pl.loop(0, m)
        def _(i):
            chunk[slot, d, i] = chunk[slot, d, i] + source[u, s, i]

    def pass_sums(u, s):
        slot = lax.rem(u, 4)

        @pl.when(c <= s)
        def _():
            if s:
                @pl.when(c > 0)
                def _():
                    arrived_right(u, s - 1).wait_recv()
                    add_to(slot, c + last - s, from_left, u, s - 1)
            sum_right(u, s).start()

        @pl.when(back <= s)
        def _():
            if s:
                @pl.when(back > 0)
                def _():
                    arrived_left(u, s - 1).wait_recv()
                    add_to(slot, c - last + s, from_right, u, s - 1)
            sum_left(u, s).start()

    def clear_sums(u):
        for s in range(last):
            @pl.when(c <= s)
            def _():
                sum_right(u, s).wait_send()

            @pl.when(back <= s)
            def _():
                sum_left(u, s).wait_send()

    def own_sum(u):
        slot = lax.rem(u, 4)

        @pl.when(c > 0)
        def _():
            arrived_right(u, last - 1).wait_recv()
            add_to(slot, c, from_left, u, last - 1)

        @pl.when(c < last)
        def _():
            arrived_left(u, last - 1).wait_recv()
            add_to(slot, c, from_right, u, last - 1)

    def spot(u):
        p, q = u // parts, lax.rem(u, parts)
        return pl.ds(pl.multiple_of(q * m, 8), m), pl.ds(pl.multiple_of(p * m, 8), m)

    def tiles(u):
        i, j = spot(u)
        return [
            pltpu.make_async_copy(state.at[i, j], tile.at[0], tile_sem.at[0]),
            pltpu.make_async_copy(gate0.at[i, j], tile.at[1], tile_sem.at[1]),
        ]

    def line_right(u, s):
        src = done.at[lax.rem(u, 2), 0] if s == 0 else line.at[c - s, u]
        send = done_sem.at[lax.rem(u, 2), 0] if s == 0 else forward_sem.at[0]
        return remote(src, line.at[c - s, u], send, line_recv_r.at[u, s], cols=c + 1)

    def line_left(u, s):
        src = done.at[lax.rem(u, 2), 0] if s == 0 else line.at[c + s, u]
        send = done_sem.at[lax.rem(u, 2), 1] if s == 0 else forward_sem.at[1]
        return remote(src, line.at[c + s, u], send, line_recv_l.at[u, s], cols=c - 1)

    def own_spread(u):
        return remote(done.at[lax.rem(u, 2), 0], lefts.at[r, u], done_sem.at[lax.rem(u, 2), 2], left_recv.at[r], rows=c)

    def own_keep(u):
        return pltpu.make_async_copy(done.at[lax.rem(u, 2), 0], line.at[c, u], done_sem.at[lax.rem(u, 2), 3])

    def right_to(u, off):
        return remote(
            done.at[lax.rem(u, 2), 1], rights.at[r, u], done_sem.at[lax.rem(u, 2), 3 + off],
            right_recv.at[r], rows=lax.rem(r + off, rows),
        )

    def kept(u):
        i, j = spot(u)
        slot = lax.rem(u, 2)
        return [
            pltpu.make_async_copy(done.at[slot, 1], rights.at[r, u], done_sem.at[slot, 7]),
            pltpu.make_async_copy(done.at[slot, 2], state1.at[i, j], done_sem.at[slot, 8]),
            pltpu.make_async_copy(done.at[slot, 3], gate1.at[i, j], done_sem.at[slot, 9]),
        ]

    def each_send(u, act):
        @pl.when(c < last)
        def _():
            act(line_right(u, 0), True)

        @pl.when(c > 0)
        def _():
            act(line_left(u, 0), True)

        @pl.when(c != r)
        def _():
            act(own_spread(u), True)

        @pl.when(c == r)
        def _():
            act(own_keep(u), False)

        for off in range(1, rows):
            act(right_to(u, off), True)
        for copy in kept(u):
            act(copy, False)

    start = lambda copy, away: copy.start()
    sent = lambda copy, away: copy.wait_send() if away else copy.wait()
    few = 8

    def update(u):
        slot, out = lax.rem(u, 4), lax.rem(u, 2)
        p, q = u // parts, lax.rem(u, parts)
        count = few * m

        @pl.loop(0, m // few)
        def _(g):
            at = pl.ds(g * few, few)
            mixed = chunk[slot, c, at].reshape(count, LANES)
            result = times(normalize(mixed, vec[0:1, :], vec[1:2, :]), out3[...])
            new = tile[0, at].reshape(count, LANES) + tile[1, at].reshape(count, LANES) * result
            normed = normalize(new, vec[2:3, :], vec[3:4, :])
            row_part = rmask[pl.ds(q * m + g * few, few)]
            col_part = cmask[pl.ds(pl.multiple_of(p * m, 8), m), :]
            mask = (row_part * col_part[None]).reshape(count, LANES)
            left, right, gating = gated_three(normed, mask, proj3[...])
            for k, value in enumerate((left, right, new, gating)):
                done[out, k, at] = value.reshape(few, m, LANES)

    def pass_line(u, s):
        @pl.when(c >= s)
        def _():
            line_right_in(u, s - 1).wait_recv()
            if s < last:
                @pl.when(c < last)
                def _():
                    line_right(u, s).start()
            spread(u, c - s)

        @pl.when(back >= s)
        def _():
            line_left_in(u, s - 1).wait_recv()
            if s < last:
                @pl.when(back < last)
                def _():
                    line_left(u, s).start()
            spread(u, c + s)

    def line_right_in(u, s):
        return remote(done.at[0, 0], line.at[c - 1 - s, u], forward_sem.at[0], line_recv_r.at[u, s], cols=c - 1)

    def line_left_in(u, s):
        return remote(done.at[0, 0], line.at[c + 1 + s, u], forward_sem.at[1], line_recv_l.at[u, s], cols=c + 1)

    def spread(u, origin):
        @pl.when(origin != r)
        def _():
            remote(line.at[origin, u], lefts.at[r, u], spread_sem, left_recv.at[r], rows=origin).start()

    def within(u):
        return jnp.logical_and(u >= 0, u < ticks)

    @pl.loop(0, ticks + 2 * last + 1)
    def _(t):
        p, q = t // parts, lax.rem(t, parts)

        @pl.when(within(t - last))
        def _():
            for copy in tiles(t - last):
                copy.start()

        @pl.when(within(t - 4))
        def _():
            clear_sums(t - 4)

        @pl.when(t < ticks)
        def _():
            @pl.when(q == 0)
            def _():
                for copy in loads(p):
                    copy.wait()
                multiply()

            turn(q, lax.rem(t, 4))
            pass_sums(t, 0)

            @pl.when(jnp.logical_and(q == 1, p + 1 < n))
            def _():
                to_across(p + 1).wait_recv()
                relay(p + 1).start()

            @pl.when(jnp.logical_and(q == parts - 1, p + 1 < n))
            def _():
                to_partner(p + 1).wait_recv()
                relay(p + 1).wait_recv()
                for copy in loads(p + 1):
                    copy.start()

        for s in range(1, last):
            @pl.when(within(t - s))
            def _():
                pass_sums(t - s, s)

        for s in range(1, last + 1):
            @pl.when(within(t - last - s))
            def _():
                pass_line(t - last - s, s)

        u = t - last

        @pl.when(within(u - 2))
        def _():
            each_send(u - 2, sent)

        @pl.when(within(u))
        def _():
            own_sum(u)
            for copy in tiles(u):
                copy.wait()
            update(u)
            each_send(u, start)

    for p in range(n):
        to_across(p).wait_send()
        to_partner(p).wait_send()
        relay(p).wait_send()

    def drain(sem, count):
        pltpu.make_async_copy(line.at[pl.ds(0, count)], line.at[pl.ds(0, count)], sem).wait()

    for count in range(1, last):
        @pl.when(c == count)
        def _():
            drain(forward_sem.at[0], count)

        @pl.when(back == count)
        def _():
            drain(forward_sem.at[1], count)

    @pl.when(c == r)
    def _():
        drain(spread_sem, last)

    @pl.when(c != r)
    def _():
        drain(spread_sem, last - 1)

    for other in range(rows):
        @pl.when(r != other)
        def _():
            pltpu.make_async_copy(lefts.at[other], lefts.at[other], left_recv.at[other]).wait()
            pltpu.make_async_copy(rights.at[other], rights.at[other], right_recv.at[other]).wait()


def middle_call(rows, cols, n, parts, left_t, right_t, state, gate0, rmask, cmask, vec, out3, proj3):
    extent = state.shape[0]
    m = extent // n
    ticks = n * parts
    last = cols - 1
    f32 = jnp.float32
    bit = (m, m, LANES)
    anywhere = pl.BlockSpec(memory_space=pl.ANY)
    inside = pl.BlockSpec(memory_space=pltpu.VMEM)
    dma = pltpu.SemaphoreType.DMA
    return pl.pallas_call(
        functools.partial(middle_kernel, rows, cols, n, parts),
        in_specs=[anywhere] * 4 + [inside] * 5,
        out_specs=[anywhere] * 6,
        out_shape=[
            jax.ShapeDtypeStruct((rows, n, LANES * m, LANES), f32),
            jax.ShapeDtypeStruct((cols, ticks) + bit, f32),
            jax.ShapeDtypeStruct((rows, ticks) + bit, f32),
            jax.ShapeDtypeStruct((rows, ticks) + bit, f32),
            jax.ShapeDtypeStruct(state.shape, f32),
            jax.ShapeDtypeStruct(state.shape, f32),
        ],
        scratch_shapes=[
            pltpu.VMEM((LANES, extent, LANES), jnp.bfloat16),
            pltpu.VMEM((LANES, extent, LANES), jnp.bfloat16),
            pltpu.VMEM((rows, LANES * m, LANES), f32),
            pltpu.VMEM((extent * LANES, LANES), f32),
            pltpu.VMEM((4, cols) + bit, f32),
            pltpu.VMEM((ticks, last) + bit, f32),
            pltpu.VMEM((ticks, last) + bit, f32),
            pltpu.VMEM((2,) + bit, f32),
            pltpu.VMEM((2, 4) + bit, f32),
            dma((3, n)), dma((3, n)), dma((4,)), dma((2,)),
            dma((4, last)), dma((4, last)), dma((ticks, last)), dma((ticks, last)),
            dma((ticks, last)), dma((ticks, last)), dma((2, 10)), dma((2,)), dma,
            dma((rows,)), dma((rows,)),
        ],
        compiler_params=pltpu.CompilerParams(
            collective_id=0, has_side_effects=True, vmem_limit_bytes=VMEM_LIMIT
        ),
    )(left_t, right_t, state, gate0, rmask, cmask, vec, out3, proj3)


def last_kernel(rows, n, parts, lefts, line, rights, state1, gate1, vec, out3, out, *scratch):
    left_k, right_k, turned = scratch[0:rows - 1], scratch[rows - 1 : 2 * rows - 2], scratch[2 * rows - 2]
    flat, load_sem = scratch[2 * rows - 1 : 2 * rows + 1]
    extent = state1.shape[0]
    m = extent // n
    r = lax.axis_index("rows")
    depth = rows * extent
    wide = depth // LANES

    def each_load(which, p, act):
        for o in range(rows):
            into = flat.at[which, pl.ds(o * extent * m, extent * m)]

            def copy(source):
                view = source.at[o, p]
                act(pltpu.make_async_copy(view, into, load_sem.at[which, o]))

            if which:
                copy(rights)
            else:
                @pl.when(r == o)
                def _():
                    copy(line)

                @pl.when(r != o)
                def _():
                    copy(lefts)

    start = lambda copy: copy.start()
    wait = lambda copy: copy.wait()
    for which in range(2):
        each_load(which, 0, start)

    @pl.loop(0, n)
    def _(p):
        for which, target in enumerate((left_k, right_k)):
            each_load(which, p, wait)

            @pl.loop(0, m)
            def _(i):
                for w in range(wide):
                    got = flat[which, pl.ds(w * LANES * m + i, LANES, m), :].T
                    target[w][pl.ds(p * m + i, LANES, extent), :] = got

            @pl.when(p + 1 < n)
            def _():
                each_load(which, p + 1, start)

    size = extent * extent
    ends = [
        pltpu.make_async_copy(source, flat.at[k, pl.ds(0, size)], load_sem.at[k, 0])
        for k, source in enumerate((state1.reshape(size, LANES), gate1.reshape(size, LANES)))
    ]
    for copy in ends:
        copy.start()

    @pl.loop(0, LANES // 2)
    def _(g):
        for b in range(2):
            h = g * 2 + b
            at = pl.ds(pl.multiple_of(h * extent, 8), extent)
            a = [halves(left_k[w][at, :]) for w in range(wide)]
            k = [halves(padded(right_k[w][at, :])) for w in range(wide)]
            a3 = jnp.concatenate([x[0] for x in a] + [x[1] for x in a] + [x[0] for x in a], axis=1)
            k3 = jnp.concatenate([x[0] for x in k] + [x[0] for x in k] + [x[1] for x in k], axis=1)
            turned[pl.ds(h, extent, LANES), :] = against(a3, k3)

    for copy in ends:
        copy.wait()

    few = 4

    @pl.loop(0, extent // few)
    def _(g):
        straight = [
            turned[pl.ds(pl.multiple_of((g * few + b) * LANES, LANES), LANES), :].T[:extent]
            for b in range(few)
        ]
        mixed = jnp.concatenate(straight, axis=0)
        result = times(normalize(mixed, vec[0:1, :], vec[1:2, :]), out3[...])
        at = pl.ds(pl.multiple_of(g * few * extent, 8), few * extent)
        out[at, :] = flat[0, at, :] + flat[1, at, :] * result


def last_call(rows, n, parts, lefts, line, rights, state1, gate1, vec, out3):
    extent = state1.shape[0]
    m = extent // n
    f32 = jnp.float32
    anywhere = pl.BlockSpec(memory_space=pl.ANY)
    inside = pl.BlockSpec(memory_space=pltpu.VMEM)
    wide = rows * extent // LANES
    pieces = lambda a: a.reshape(rows, n, parts * m * m, LANES)
    out = pl.pallas_call(
        functools.partial(last_kernel, rows, n, parts),
        in_specs=[anywhere] * 5 + [inside] * 2,
        out_specs=inside,
        out_shape=jax.ShapeDtypeStruct((extent * extent, LANES), f32),
        scratch_shapes=[pltpu.VMEM((LANES * extent, LANES), f32)] * (2 * wide + 1)
        + [pltpu.VMEM((2, rows * extent * m, LANES), f32), pltpu.SemaphoreType.DMA((2, rows))],
        compiler_params=pltpu.CompilerParams(vmem_limit_bytes=VMEM_LIMIT),
    )(pieces(lefts), pieces(line), pieces(rights), state1, gate1, vec, out3)
    return out.reshape(extent, extent, LANES)


def body(rows, cols, pieces, pair_state, token_mask, norm_gain, norm_bias, proj_weight,
         gate_weight, out_gain, out_bias, out_weight):
    extent = pair_state.shape[0]
    row_at, col_at = lax.axis_index("rows"), lax.axis_index("cols")
    maskf = token_mask.astype(jnp.float32)
    spread = lambda at: jnp.broadcast_to(
        lax.dynamic_slice_in_dim(maskf, at * extent, extent)[:, None], (extent, LANES)
    )
    rmask, cmask = spread(row_at)[:, None, :], spread(col_at)
    full = jnp.concatenate([proj_weight, gate_weight], axis=2)
    left_t, right_t, gate0 = first_call(
        pieces, pair_state, rmask, cmask, jnp.stack([norm_gain[0], norm_bias[0]]), stacked(full[0])
    )
    _, line, lefts, rights, state1, gate1 = middle_call(
        rows, cols, pieces, pieces, left_t, right_t, pair_state, gate0, rmask, cmask,
        jnp.stack([out_gain[0], out_bias[0], norm_gain[1], norm_bias[1]]),
        stacked(out_weight[0]), stacked(full[1]),
    )
    return last_call(
        rows, pieces, pieces, lefts, line, rights, state1, gate1,
        jnp.stack([out_gain[1], out_bias[1]]), stacked(out_weight[1]),
    )


def solution(mesh):
    placed = (P(("groups", "rows"), "cols", None), P("groups"), P(), P(), P(), P(), P(), P(), P())
    rows, cols = mesh.shape["rows"], mesh.shape["cols"]

    def run(pair_state, *rest):
        proj_weight = rest[3]
        channels, hidden = pair_state.shape[2], proj_weight.shape[2] // 4
        extent = pair_state.shape[0]
        fits = channels == hidden == LANES and extent == pair_state.shape[1] and extent <= LANES
        if rows == cols == 4 and fits and extent % (8 * rows) == 0:
            return body(rows, cols, rows, pair_state, *rest)
        return plain_body(pair_state, *rest)

    return jax.shard_map(
        run,
        mesh=mesh,
        in_specs=placed,
        out_specs=P(("groups", "rows"), "cols", None),
        check_vma=False,
    )
```

profile of v0, /device:TPU:1, one launch (start us, length us, event | category | flops | bytes accessed | tf_op | source)
XLA Modules:
  0.0 671.1 jit_solution(15781299758689028428)
XLA Ops:
  0.0 0.7 convert_element_type.27
  0.7 0.1 fusion.4
  0.8 0.8 fusion.7
  1.5 0.5 pad_maximum_fusion.5.vec
  2.1 0.8 fusion.5
  2.8 0.6 pad_maximum_fusion.6.vec
  3.4 0.6 pad_maximum_fusion.4.vec
  4.0 0.7 broadcast_in_dim.2.cmask
  4.7 0.8 broadcast_in_dim_broadcast_in_dim.2.rmask
  5.5 0.9 reduce-precision_convert_fusion.2
  6.4 0.7 pad_maximum_fusion.2
  7.1 1.1 constant_dynamic-update-slice_fusion.1
  8.1 0.9 constant_dynamic-update-slice_fusion
  9.1 0.1 reduce-precision_convert_fusion
  9.2 1.0 pad_maximum_fusion
  10.2 20.8 %shard_map.91 = (f32[4,3072,128]{2,1,0:T(8,128)}, f32[4,3072,128]{2,1,0:T(8,128)}, f32[96,96,128]{2,1,0:T(8,128)}) custom-call(f32[96,96,128]{2,1,0:T(8,128)} %state.3, f32[96,1,128]{2,1,0:T(1,128)} %broadcast_in_dim_broadcast_in_dim.2.rmask, f32[96,128]{1,0:T(8,128)} %broadcast_in_dim.2.cmask, f32[2,128]{1,0:T(2,128)} %pad_maximum_fusion.5.vec, ...), custom_call_target="tpu_custom_call" | custom-call | tf_op jit(solution)/shard_map/pallas_call | solution.py:168
  31.0 547.5 %shard_map.92 = (f32[4,4,3072,128]{3,2,1,0:T(8,128)}, f32[4,16,24,24,128]{4,3,2,1,0:T(8,128)}, f32[4,16,24,24,128]{4,3,2,1,0:T(8,128)}, f32[4,16,24,24,128]{4,3,...) custom-call(f32[4,3072,128]{2,1,0:T(8,128)} %get-tuple-element.13.left_t, ...), custom_call_target="tpu_custom_call" | custom-call | tf_op jit(solution)/shard_map/pallas_call | solution.py:574
  578.6 92.6 %shard_map.93 = f32[9216,128]{1,0:T(8,128)} custom-call(f32[4,4,2304,128]{3,2,1,0:T(8,128)} %bitcast.23, f32[4,4,2304,128]{3,2,1,0:T(8,128)} %bitcast.22, f32[4,4,2304,128]{3,2,1,0:T(8,128)} %bitcast.24, f32[96,96,128]{2,1,0:T(8,128)} %get-tuple-element.19.state1, f32[96,96,128]{2,1,0:T(8,128)} %get-tuple-element.20.gate1, f32[2,128]{1,0:T(2,128)} %pad_maximum_fusion.6.vec, ...), custom_call_target="tpu_custom_call" | custom-call | tf_op jit(solution)/shard_map/pallas_call | solution.py:699
where the time goes:
time: 671 us
  Pallas kernels  661 us (99%)
    pallas_call x1, Pallas kernels, middle_call(): pl.pallas_call(functools.partial(middle_kernel, rows, cols, n, parts), in...  548 us
    pallas_call x1, Pallas kernels, last_call(): pl.pallas_call(functools.partial(last_kernel, rows, n, parts), in_specs=[...  92.6 us
    pallas_call x1, Pallas kernels, first_call(): pl.pallas_call(functools.partial(first_kernel, 4), grid=(n,), in_specs=[p...  20.8 us

commit v1 on v0

v1 whole, which is shorter than its diff:
```python
import functools

import jax
import jax.numpy as jnp
from jax import lax
from jax.experimental import pallas as pl
from jax.experimental.pallas import tpu as pltpu
from jax.sharding import PartitionSpec as P

eps = 1e-05
precise = lax.Precision.HIGH
MESH = pl.DeviceIdType.MESH
LANES = 128
VMEM_LIMIT = 67_000_000


def normalize(values, gain, shift):
    center = values - jnp.mean(values, axis=-1, keepdims=True)
    spread = jnp.mean(center * center, axis=-1, keepdims=True)
    return center * lax.rsqrt(spread + eps) * gain + shift


def project(state, pair_mask, segment, norm_gain, norm_bias, proj_weight, gate_weight):
    width = proj_weight.shape[2] // 4
    normed = normalize(state, norm_gain[segment], norm_bias[segment])
    hidden = jnp.einsum(
        "ijc,cf->ijf", normed, proj_weight[segment], precision=precise
    )
    left_side = (
        pair_mask[:, :, None]
        * jax.nn.sigmoid(hidden[:, :, :width])
        * hidden[:, :, width : 2 * width]
    )
    right_side = (
        pair_mask[:, :, None]
        * jax.nn.sigmoid(hidden[:, :, 2 * width : 3 * width])
        * hidden[:, :, 3 * width :]
    )
    gating = jax.nn.sigmoid(
        jnp.einsum("ijc,cd->ijd", normed, gate_weight[segment], precision=precise)
    )
    return (left_side, right_side, gating)


def finish(state, mixed, gating, segment, out_gain, out_bias, out_weight):
    result = jnp.einsum(
        "ijh,hc->ijc",
        normalize(mixed, out_gain[segment], out_bias[segment]),
        out_weight[segment],
        precision=precise,
    )
    return state + gating * result


def plain_body(
    pair_state,
    token_mask,
    norm_gain,
    norm_bias,
    proj_weight,
    gate_weight,
    out_gain,
    out_bias,
    out_weight,
):
    row_count = pair_state.shape[0]
    col_count = pair_state.shape[1]
    row_start = lax.axis_index("rows") * row_count
    col_start = lax.axis_index("cols") * col_count
    maskf = token_mask.astype(jnp.float32)
    row_mask = lax.dynamic_slice_in_dim(maskf, row_start, row_count)
    col_mask = lax.dynamic_slice_in_dim(maskf, col_start, col_count)
    pair_mask = row_mask[:, None] * col_mask[None, :]
    left_side, right_side, gating = project(
        pair_state, pair_mask, 0, norm_gain, norm_bias, proj_weight, gate_weight
    )
    partial_out = jnp.einsum(
        "ikh,jkh->ijh",
        left_side,
        lax.all_gather(right_side, "rows", axis=0, tiled=True),
        precision=precise,
    )
    mixed = lax.psum_scatter(partial_out, "cols", scatter_dimension=1, tiled=True)
    updated = finish(pair_state, mixed, gating, 0, out_gain, out_bias, out_weight)
    left_next, right_next, gate_next = project(
        updated, pair_mask, 1, norm_gain, norm_bias, proj_weight, gate_weight
    )
    partial_in = jnp.einsum(
        "kih,kjh->ijh",
        lax.all_gather(left_next, "cols", axis=1, tiled=True),
        right_next,
        precision=precise,
    )
    mixed_next = lax.psum_scatter(partial_in, "rows", scatter_dimension=0, tiled=True)
    return finish(updated, mixed_next, gate_next, 1, out_gain, out_bias, out_weight)


def halves(x):
    high = x.astype(jnp.bfloat16)
    return high, (x - high.astype(jnp.float32)).astype(jnp.bfloat16)


def streamed(x):
    high, low = halves(x)
    return jnp.concatenate([high, low, high], axis=1)


def held(x):
    high, low = halves(x)
    return jnp.concatenate([high, high, low], axis=1)


def stack_into(target, first, weight):
    high, low = halves(weight)
    for k, part in enumerate((high, high, low)):
        target[k * LANES : (k + 1) * LANES, first : first + weight.shape[1]] = part


def times(x, weight3):
    return jnp.dot(streamed(x), weight3, preferred_element_type=jnp.float32)


def against(a3, b3):
    return lax.dot_general(
        a3, b3, (((1,), (1,)), ((), ())), preferred_element_type=jnp.float32
    )


def gated_three(normed, mask, weight3):
    hidden = times(normed, weight3)
    part = lambda f: hidden[:, f * LANES : (f + 1) * LANES]
    return (
        mask * jax.nn.sigmoid(part(0)) * part(1),
        mask * jax.nn.sigmoid(part(2)) * part(3),
        jax.nn.sigmoid(part(4)),
    )


def padded(x):
    rows = x.shape[0]
    if rows == LANES:
        return x
    return jnp.concatenate([x, jnp.zeros((LANES - rows, x.shape[1]), x.dtype)], axis=0)


def middle_kernel(
    rows, cols, n, parts,
    state, tokens, norm_gain, norm_bias, proj, gate_weight, out_gain, out_bias, out_weight,
    near, line, lefts, rights, right_k, state1, gate1, gate0,
    mine, first, opened, first3, high, low, block, turned, stage, chunk, from_left, from_right, tile, done, ready, out3, proj3,
    first_sem, opened_sem, early_send, early_recv, gather_send, gather_recv, load_sem, tile_sem,
    sum_send_r, sum_send_l, sum_recv_r, sum_recv_l,
    line_recv_r, line_recv_l, done_sem, forward_sem, spread_sem, left_recv,
    right_near, right_across, right_beyond, right_relay, stage_sem,
):
    mi, m = tile.shape[1:3]
    extent = n * m
    ticks = n * parts
    last = cols - 1
    r, c = lax.axis_index("rows"), lax.axis_index("cols")
    back = last - c
    depth, ring = done.shape[0], from_left.shape[0]
    partner = r + 1 - 2 * lax.rem(r, 2)
    across = lax.rem(r + 2, rows)
    beyond = lax.rem(partner + 2, rows)

    def opening(p):
        return pltpu.make_async_copy(state.at[pl.ds(p * m, m)], first.at[p % 2], first_sem.at[p % 2])

    opening(0).start()
    stack_into(first3, 0, proj[0])
    stack_into(first3, 4 * LANES, gate_weight[0])
    stack_into(out3, 0, out_weight[0])
    stack_into(proj3, 0, proj[1])
    stack_into(proj3, 4 * LANES, gate_weight[1])

    barrier = pltpu.get_barrier_semaphore()
    for off in range(1, rows):
        pl.semaphore_signal(barrier, inc=1, device_id={"rows": lax.rem(r + off, rows)}, device_id_type=MESH)

    @pl.when(c > 0)
    def _():
        pl.semaphore_signal(barrier, inc=1, device_id={"cols": c - 1}, device_id_type=MESH)

    @pl.when(c < last)
    def _():
        pl.semaphore_signal(barrier, inc=1, device_id={"cols": c + 1}, device_id_type=MESH)

    pl.semaphore_wait(barrier, rows - 1 + jnp.minimum(c, 1) + jnp.minimum(back, 1))

    def remote(src, dst, send, recv, **where):
        return pltpu.make_async_remote_copy(
            src_ref=src, dst_ref=dst, send_sem=send, recv_sem=recv,
            device_id=where, device_id_type=MESH,
        )

    def to_partner(p):
        return remote(mine.at[p], near.at[0, p], gather_send.at[0, p], gather_recv.at[0, p], rows=partner)

    def to_across(p):
        return remote(mine.at[p], near.at[1, p], gather_send.at[1, p], gather_recv.at[1, p], rows=across)

    def relay(p):
        return remote(near.at[1, p], near.at[2, p], gather_send.at[2, p], gather_recv.at[2, p], rows=partner)

    def slab(o):
        return block.at[pl.ds(pl.multiple_of(o * LANES * m, 8), LANES * m)]

    def loads(p):
        return [
            pltpu.make_async_copy(mine.at[p], slab(r), load_sem.at[0]),
            pltpu.make_async_copy(near.at[0, p], slab(partner), load_sem.at[1]),
            pltpu.make_async_copy(near.at[1, p], slab(across), load_sem.at[2]),
            pltpu.make_async_copy(near.at[2, p], slab(beyond), load_sem.at[3]),
        ]

    cuts = 4
    cut = LANES // cuts

    def part(k):
        return pl.ds(k * cut * m, cut * m)

    def early(k):
        return (
            remote(mine.at[0, part(k)], near.at[0, 0, part(k)], early_send.at[0, k], early_recv.at[0, k], rows=partner),
            remote(mine.at[0, part(k)], near.at[1, 0, part(k)], early_send.at[1, k], early_recv.at[1, k], rows=across),
            remote(near.at[1, 0, part(k)], near.at[2, 0, part(k)], early_send.at[2, k], early_recv.at[2, k], rows=partner),
        )

    def early_loads(k):
        return [
            pltpu.make_async_copy(
                source.at[0, part(k)],
                block.at[pl.ds(pl.multiple_of(o * LANES * m + k * cut * m, 8), cut * m)],
                load_sem.at[b],
            )
            for b, (source, o) in enumerate(
                ((mine, r), (near.at[0], partner), (near.at[1], across), (near.at[2], beyond))
            )
        ]

    def closing(p):
        return pltpu.make_async_copy(opened.at[p % 2], gate0.at[pl.ds(p * m, m)], opened_sem.at[p % 2])

    group = 4
    taken = group * extent
    for p in range(n):
        opening(p).wait()
        if p + 1 < n:
            opening(p + 1).start()
        if p >= 2:
            closing(p - 2).wait()

        @pl.loop(0, m // group)
        def _(g):
            rows_at = pl.ds(g * group, group)
            normed = normalize(first[p % 2, rows_at].reshape(taken, LANES), norm_gain[0:1, :], norm_bias[0:1, :])
            row_first = r * extent + p * m + g * group
            col_part = tokens[pl.ds(pl.multiple_of(c * extent, 8), extent), :]
            mask = jnp.concatenate(
                [tokens[pl.ds(row_first + b, 1), :] * col_part for b in range(group)], axis=0
            )
            left, right, gating = gated_three(normed, mask, first3[...])
            opened[p % 2, rows_at] = gating.reshape(group, extent, LANES)
            for b in range(group):
                span = slice(b * extent, (b + 1) * extent)
                mine[p, pl.ds(g * group + b, LANES, m), :] = padded(right[span]).T
                turned[1, pl.ds(p * LANES * m + g * group + b, LANES, m), :] = padded(left[span]).T

        closing(p).start()
        if p:
            to_across(p).start()
            to_partner(p).start()
        else:
            for k in range(cuts):
                for copy in early(k)[1::-1]:
                    copy.start()
    for p in range(max(n - 2, 0), n):
        closing(p).wait()

    @pl.loop(0, LANES)
    def _(h):
        rows_of = [
            turned[1, pl.ds(pl.multiple_of(p * LANES * m + h * m, 8), m), :] for p in range(n)
        ]
        top, rest = halves(jnp.concatenate(rows_of, axis=0))
        high[h] = top
        low[h] = rest

    def multiply(p, start_at, count):
        half = lax.rem(p, 2)

        @pl.loop(start_at // 4, (start_at + count) // 4)
        def _(g):
            for b in range(4):
                h = g * 4 + b
                right = padded(jnp.concatenate(
                    [block[pl.ds(pl.multiple_of(o * LANES * m + h * m, 8), m), :] for o in range(rows)], axis=0
                ))
                a3 = jnp.concatenate([high[h], low[h], high[h]], axis=1)
                turned[half, pl.ds(h, extent, LANES), :] = against(a3, held(right))

    def turn(p, q, slot):
        @pl.loop(0, mi)
        def _(i):
            at = pl.multiple_of((q * mi + i) * LANES, LANES)
            straight = turned[lax.rem(p, 2), pl.ds(at, LANES), :].T
            for d in range(cols):
                chunk[slot, d, i] = straight[d * m : (d + 1) * m]

    def sum_right(u, s):
        slot = lax.rem(u, 4)
        return remote(chunk.at[slot, c + last - s], from_left.at[lax.rem(u, ring), s], sum_send_r.at[slot, s], sum_recv_r.at[lax.rem(u, ring), s], cols=c + 1)

    def sum_left(u, s):
        slot = lax.rem(u, 4)
        return remote(chunk.at[slot, c - last + s], from_right.at[lax.rem(u, ring), s], sum_send_l.at[slot, s], sum_recv_l.at[lax.rem(u, ring), s], cols=c - 1)

    def arrived_right(u, s):
        return remote(chunk.at[0, 0], from_left.at[lax.rem(u, ring), s], sum_send_r.at[0, s], sum_recv_r.at[lax.rem(u, ring), s], cols=c - 1)

    def arrived_left(u, s):
        return remote(chunk.at[0, 0], from_right.at[lax.rem(u, ring), s], sum_send_l.at[0, s], sum_recv_l.at[lax.rem(u, ring), s], cols=c + 1)

    def add_to(slot, d, source, u, s):
        @pl.loop(0, mi)
        def _(i):
            chunk[slot, d, i] = chunk[slot, d, i] + source[lax.rem(u, ring), s, i]

    def pass_sums(u, s):
        slot = lax.rem(u, 4)

        @pl.when(c <= s)
        def _():
            if s:
                @pl.when(c > 0)
                def _():
                    arrived_right(u, s - 1).wait_recv()
                    add_to(slot, c + last - s, from_left, u, s - 1)
            sum_right(u, s).start()

        @pl.when(back <= s)
        def _():
            if s:
                @pl.when(back > 0)
                def _():
                    arrived_left(u, s - 1).wait_recv()
                    add_to(slot, c - last + s, from_right, u, s - 1)
            sum_left(u, s).start()

    def clear_sums(u):
        for s in range(last):
            @pl.when(c <= s)
            def _():
                sum_right(u, s).wait_send()

            @pl.when(back <= s)
            def _():
                sum_left(u, s).wait_send()

    def own_sum(u):
        slot = lax.rem(u, 4)

        @pl.when(c > 0)
        def _():
            arrived_right(u, last - 1).wait_recv()
            add_to(slot, c, from_left, u, last - 1)

        @pl.when(c < last)
        def _():
            arrived_left(u, last - 1).wait_recv()
            add_to(slot, c, from_right, u, last - 1)

    def spot(u):
        p, q = u // parts, lax.rem(u, parts)
        return pl.ds(q * mi, mi), pl.ds(pl.multiple_of(p * m, 8), m)

    def tiles(u):
        i, j = spot(u)
        return [
            pltpu.make_async_copy(state.at[i, j], tile.at[0], tile_sem.at[0]),
            pltpu.make_async_copy(gate0.at[i, j], tile.at[1], tile_sem.at[1]),
        ]

    def at(u):
        return pl.ds(pl.multiple_of(u * mi * m, 8), mi * m)

    def line_right(u, s):
        src = done.at[lax.rem(u, depth), 0] if s == 0 else line.at[c - s, at(u)]
        send = done_sem.at[lax.rem(u, depth), 0] if s == 0 else forward_sem.at[0]
        return remote(src, line.at[c - s, at(u)], send, line_recv_r.at[u, s], cols=c + 1)

    def line_left(u, s):
        src = done.at[lax.rem(u, depth), 0] if s == 0 else line.at[c + s, at(u)]
        send = done_sem.at[lax.rem(u, depth), 1] if s == 0 else forward_sem.at[1]
        return remote(src, line.at[c + s, at(u)], send, line_recv_l.at[u, s], cols=c - 1)

    def own_spread(u):
        return remote(done.at[lax.rem(u, depth), 0], lefts.at[r, at(u)], done_sem.at[lax.rem(u, depth), 2], left_recv.at[r, u // parts], rows=c)

    def own_keep(u):
        return pltpu.make_async_copy(done.at[lax.rem(u, depth), 0], line.at[c, at(u)], done_sem.at[lax.rem(u, depth), 3])

    def right_to_partner(u):
        return remote(done.at[lax.rem(u, depth), 1], rights.at[r, at(u)], done_sem.at[lax.rem(u, depth), 4], right_near.at[u // parts], rows=partner)

    def right_to_across(u):
        return remote(done.at[lax.rem(u, depth), 1], rights.at[r, at(u)], done_sem.at[lax.rem(u, depth), 5], right_across.at[u], rows=across)

    def right_on(u):
        return remote(rights.at[across, at(u)], rights.at[across, at(u)], right_relay, right_beyond.at[u // parts], rows=partner)

    def kept(u):
        i, j = spot(u)
        slot = lax.rem(u, depth)
        return [
            pltpu.make_async_copy(done.at[slot, 1], rights.at[r, at(u)], done_sem.at[slot, 6]),
            pltpu.make_async_copy(ready.at[slot, 0], state1.at[i, j], done_sem.at[slot, 7]),
            pltpu.make_async_copy(ready.at[slot, 1], gate1.at[i, j], done_sem.at[slot, 8]),
        ]

    def each_send(u, act):
        @pl.when(c < last)
        def _():
            act(line_right(u, 0), True)

        @pl.when(c > 0)
        def _():
            act(line_left(u, 0), True)

        @pl.when(c != r)
        def _():
            act(own_spread(u), True)

        @pl.when(c == r)
        def _():
            act(own_keep(u), False)

        act(right_to_across(u), True)
        act(right_to_partner(u), True)
        for copy in kept(u):
            act(copy, False)

    start = lambda copy, away: copy.start()
    sent = lambda copy, away: copy.wait_send() if away else copy.wait()
    few = next(k for k in (8, 6, 4, 3, 2, 1) if mi % k == 0)

    def update(u):
        slot, out = lax.rem(u, 4), lax.rem(u, depth)
        p, q = u // parts, lax.rem(u, parts)
        count = few * m

        @pl.loop(0, mi // few)
        def _(g):
            rows_at = pl.ds(g * few, few)
            mixed = chunk[slot, c, rows_at].reshape(count, LANES)
            result = times(normalize(mixed, out_gain[0:1, :], out_bias[0:1, :]), out3[...])
            new = tile[0, rows_at].reshape(count, LANES) + tile[1, rows_at].reshape(count, LANES) * result
            normed = normalize(new, norm_gain[1:2, :], norm_bias[1:2, :])
            row_first = r * extent + q * mi + g * few
            col_part = tokens[pl.ds(pl.multiple_of(c * extent + p * m, 8), m), :]
            mask = jnp.concatenate(
                [tokens[pl.ds(row_first + b, 1), :] * col_part for b in range(few)], axis=0
            )
            left, right, gating = gated_three(normed, mask, proj3[...])
            for k, value in enumerate((left, right)):
                done[out, k, pl.ds(pl.multiple_of(g * count, 8), count), :] = value
            for k, value in enumerate((new, gating)):
                ready[out, k, rows_at] = value.reshape(few, m, LANES)

    def pass_line(u, s):
        @pl.when(c >= s)
        def _():
            line_right_in(u, s - 1).wait_recv()
            if s < last:
                @pl.when(c < last)
                def _():
                    line_right(u, s).start()
            spread(u, c - s)

        @pl.when(back >= s)
        def _():
            line_left_in(u, s - 1).wait_recv()
            if s < last:
                @pl.when(back < last)
                def _():
                    line_left(u, s).start()
            spread(u, c + s)

    def line_right_in(u, s):
        return remote(done.at[0, 0], line.at[c - 1 - s, at(u)], forward_sem.at[0], line_recv_r.at[u, s], cols=c - 1)

    def line_left_in(u, s):
        return remote(done.at[0, 0], line.at[c + 1 + s, at(u)], forward_sem.at[1], line_recv_l.at[u, s], cols=c + 1)

    def spread(u, origin):
        @pl.when(origin != r)
        def _():
            remote(
                line.at[origin, at(u)], lefts.at[r, at(u)], spread_sem, left_recv.at[r, u // parts], rows=origin
            ).start()

    wide = rows * extent // LANES
    share = extent * m

    def piece(p):
        return pl.ds(p * share, share)

    def fetch(which, p):
        span = piece(p)
        for o in range(rows):
            if which:
                pltpu.make_async_copy(rights.at[o, span], fetched(o), load_sem.at[o]).start()
            else:
                @pl.when(r == o)
                def _():
                    pltpu.make_async_copy(line.at[o, span], fetched(o), load_sem.at[o]).start()

                @pl.when(r != o)
                def _():
                    pltpu.make_async_copy(lefts.at[o, span], fetched(o), load_sem.at[o]).start()

    def fetched(o):
        return block.at[pl.ds(o * share, share)]

    def arrived(which, p):
        span = piece(p)

        def settle(ref, o, sem):
            pltpu.make_async_copy(ref.at[o, span], ref.at[o, span], sem).wait()

        if which:
            settle(rights, partner, right_near.at[p])
            settle(rights, beyond, right_beyond.at[p])
        else:
            for o in range(rows):
                @pl.when(r != o)
                def _():
                    settle(lefts, o, left_recv.at[o, p])

    def put(which, p):
        target = right_k if which else near
        return [pltpu.make_async_copy(stage.at[w], target.at[w, p], stage_sem.at[w]) for w in range(wide)]

    def along(which, p, before):
        for o in range(rows):
            pltpu.make_async_copy(rights.at[o, piece(p)], fetched(o), load_sem.at[o]).wait()
        if before is not None:
            for copy in put(*before):
                copy.wait()

        @pl.loop(0, m)
        def _(i):
            for w in range(wide):
                got = block[pl.ds(w * LANES * m + i, LANES, m), :].T
                stage[w, pl.ds(i, LANES, m), :] = got

        for copy in put(which, p):
            copy.start()

    def within(u):
        return jnp.logical_and(u >= 0, u < ticks)

    order = [(0, p) for p in range(n)] + [(1, p) for p in range(n)]
    late = 4
    known = lambda which, p: (p + 1) * parts - 1 + last + max(late + 2, depth)
    turns = ticks + last + max(depth, late, last + 1)
    order.sort(key=lambda step: known(*step))
    begins = []
    for step in order:
        begins.append(max(known(*step), begins[-1] + 1 if begins else ticks - parts))
    steps, ending = [], []
    for k, (which, p) in enumerate(order):
        before = order[k - 1] if k else None

        def begin(which=which, p=p):
            arrived(which, p)
            fetch(which, p)

        def close(which=which, p=p, before=before):
            along(which, p, before)

        for when, act in ((begins[k], begin), (begins[k] + 1, close)):
            if when < turns:
                steps.append((when, act))
            else:
                ending.append(act)
    steps.sort(key=lambda step: step[0])

    half_way = parts // 2
    some = LANES // (parts - half_way)
    for k in range(cuts):
        near_copy, far_copy, on_copy = early(k)
        far_copy.wait_recv()
        on_copy.start()
        near_copy.wait_recv()
        on_copy.wait_recv()
        for copy in early_loads(k):
            copy.start()
        for copy in early_loads(k):
            copy.wait()
        multiply(0, k * cut, cut)
    for k in range(cuts):
        for copy in early(k):
            copy.wait_send()

    @pl.loop(0, turns)
    def _(t):
        p, q = t // parts, lax.rem(t, parts)

        @pl.when(within(t - last))
        def _():
            for copy in tiles(t - last):
                copy.start()

        @pl.when(within(t - 4))
        def _():
            clear_sums(t - 4)

        @pl.when(t < ticks)
        def _():
            turn(p, q, lax.rem(t, 4))
            pass_sums(t, 0)

            @pl.when(p + 1 < n)
            def _():
                @pl.when(q == half_way - 2)
                def _():
                    to_across(p + 1).wait_recv()
                    relay(p + 1).start()

                @pl.when(q == half_way - 1)
                def _():
                    to_partner(p + 1).wait_recv()
                    relay(p + 1).wait_recv()
                    for copy in loads(p + 1):
                        copy.start()

                @pl.when(q == half_way)
                def _():
                    relay(p + 1).wait_send()
                    for copy in loads(p + 1):
                        copy.wait()

                @pl.when(q >= half_way)
                def _():
                    multiply(p + 1, (q - half_way) * some, some)

        for s in range(1, last):
            @pl.when(within(t - s))
            def _():
                pass_sums(t - s, s)

        for s in range(1, last + 1):
            @pl.when(within(t - last - s))
            def _():
                pass_line(t - last - s, s)

        u = t - last

        @pl.when(within(u - late))
        def _():
            right_to_across(u - late).wait_recv()
            right_on(u - late).start()

        @pl.when(within(u - depth))
        def _():
            each_send(u - depth, sent)

        for when, act in steps:
            @pl.when(t == when)
            def _():
                act()

        @pl.when(within(u))
        def _():
            own_sum(u)
            for copy in tiles(u):
                copy.wait()
            update(u)
            each_send(u, start)

    for act in ending:
        act()
    for copy in put(*order[-1]):
        copy.wait()
    for p in range(1, n):
        to_across(p).wait_send()
        to_partner(p).wait_send()

    def drain(sem, count):
        pltpu.make_async_copy(line.at[pl.ds(0, count)], line.at[pl.ds(0, count)], sem).wait()

    for count in range(1, last):
        @pl.when(c == count)
        def _():
            drain(forward_sem.at[0], count)

        @pl.when(back == count)
        def _():
            drain(forward_sem.at[1], count)

    drain(right_relay, 1)

    @pl.when(c == r)
    def _():
        drain(spread_sem, last)

    @pl.when(c != r)
    def _():
        drain(spread_sem, last - 1)


def middle_call(rows, cols, n, parts, state, *small):
    extent = state.shape[0]
    m, mi = extent // n, extent // parts
    ticks = n * parts
    last = cols - 1
    wide = rows * extent // LANES
    f32, bf16 = jnp.float32, jnp.bfloat16
    bit, flat = (mi, m, LANES), (mi * m, LANES)
    anywhere = pl.BlockSpec(memory_space=pl.ANY)
    inside = pl.BlockSpec(memory_space=pltpu.VMEM)
    dma = pltpu.SemaphoreType.DMA
    whole = jax.ShapeDtypeStruct((rows, extent * extent, LANES), f32)
    long = jax.ShapeDtypeStruct((wide, n, LANES * m, LANES), f32)
    square = jax.ShapeDtypeStruct(state.shape, f32)
    return pl.pallas_call(
        functools.partial(middle_kernel, rows, cols, n, parts),
        in_specs=[anywhere] + [inside] * len(small),
        out_specs=[anywhere] * 8,
        out_shape=[long, whole, whole, whole, long, square, square, square],
        scratch_shapes=[
            pltpu.VMEM((n, LANES * m, LANES), f32),
            pltpu.VMEM((2, m, extent, LANES), f32),
            pltpu.VMEM((2, m, extent, LANES), f32),
            pltpu.VMEM((3 * LANES, 5 * LANES), bf16),
            pltpu.VMEM((LANES, extent, LANES), bf16),
            pltpu.VMEM((LANES, extent, LANES), bf16),
            pltpu.VMEM((rows * max(LANES, extent) * m, LANES), f32),
            pltpu.VMEM((2, extent * LANES, LANES), f32),
            pltpu.VMEM((wide, LANES * m, LANES), f32),
            pltpu.VMEM((4, cols) + bit, f32),
            pltpu.VMEM((6, last) + bit, f32),
            pltpu.VMEM((6, last) + bit, f32),
            pltpu.VMEM((2,) + bit, f32),
            pltpu.VMEM((8, 2) + flat, f32),
            pltpu.VMEM((8, 2) + bit, f32),
            pltpu.VMEM((3 * LANES, LANES), bf16),
            pltpu.VMEM((3 * LANES, 5 * LANES), bf16),
            dma((2,)), dma((2,)), dma((3, 4)), dma((3, 4)), dma((3, n)), dma((3, n)), dma((max(n, rows),)), dma((2,)),
            dma((4, last)), dma((4, last)), dma((6, last)), dma((6, last)),
            dma((ticks, last)), dma((ticks, last)), dma((8, 9)), dma((2,)), dma,
            dma((rows, n)), dma((n,)), dma((ticks,)), dma((n,)), dma, dma((wide,)),
        ],
        compiler_params=pltpu.CompilerParams(
            collective_id=0, has_side_effects=True, vmem_limit_bytes=VMEM_LIMIT
        ),
    )(state, *small)


def last_kernel(left_k, right_k, state1, gate1, out_gain, out_bias, out_weight, out, turned, ends, out3, end_sem):
    g, steps = pl.program_id(0), pl.num_programs(0)
    wide, n, block, _ = left_k.shape
    size = ends.shape[1]
    extent = turned.shape[0] // LANES
    m = extent // n
    heads = block // m
    copies = [pltpu.make_async_copy(source, ends.at[k], end_sem.at[k]) for k, source in enumerate((state1, gate1))]

    @pl.when(g == 0)
    def _():
        for copy in copies:
            copy.start()
        stack_into(out3, 0, out_weight[1])

    def rows_of(ref, b, w):
        return jnp.concatenate([ref[w, p, b * m : (b + 1) * m, :] for p in range(n)], axis=0)

    for b in range(heads):
        a = [halves(rows_of(left_k, b, w)) for w in range(wide)]
        k = [halves(padded(rows_of(right_k, b, w))) for w in range(wide)]
        a3 = jnp.concatenate([x[0] for x in a] + [x[1] for x in a] + [x[0] for x in a], axis=1)
        k3 = jnp.concatenate([x[0] for x in k] + [x[0] for x in k] + [x[1] for x in k], axis=1)
        turned[pl.ds(g * heads + b, extent, LANES), :] = against(a3, k3)

    @pl.when(g == steps - 1)
    def _():
        for copy in copies:
            copy.wait()
        few = 4

        @pl.loop(0, extent // few)
        def _(i):
            straight = [
                turned[pl.ds(pl.multiple_of((i * few + b) * LANES, LANES), LANES), :].T[:extent]
                for b in range(few)
            ]
            mixed = jnp.concatenate(straight, axis=0)
            result = times(normalize(mixed, out_gain[1:2, :], out_bias[1:2, :]), out3[...])
            at = pl.ds(pl.multiple_of(i * few * extent, 8), few * extent)
            out[at, :] = ends[0, at, :] + ends[1, at, :] * result


def last_call(left_k, right_k, state1, gate1, *small):
    extent = state1.shape[0]
    wide, n, _, _ = left_k.shape
    size = extent * extent
    f32 = jnp.float32
    heads = 8
    part = pl.BlockSpec((wide, n, heads * (extent // n), LANES), lambda g: (0, 0, g, 0))
    anywhere = pl.BlockSpec(memory_space=pl.ANY)
    out = pl.pallas_call(
        last_kernel,
        grid=(LANES // heads,),
        in_specs=[part, part, anywhere, anywhere]
        + [pl.BlockSpec(a.shape, lambda g, a=a: (0,) * a.ndim) for a in small],
        out_specs=pl.BlockSpec((size, LANES), lambda g: (0, 0)),
        out_shape=jax.ShapeDtypeStruct((size, LANES), f32),
        scratch_shapes=[
            pltpu.VMEM((extent * LANES, LANES), f32),
            pltpu.VMEM((2, size, LANES), f32),
            pltpu.VMEM((3 * LANES, LANES), jnp.bfloat16),
            pltpu.SemaphoreType.DMA((2,)),
        ],
        compiler_params=pltpu.CompilerParams(vmem_limit_bytes=VMEM_LIMIT),
    )(left_k, right_k, state1.reshape(size, LANES), gate1.reshape(size, LANES), *small)
    return out.reshape(extent, extent, LANES)


def body(rows, cols, pieces, parts, pair_state, token_mask, norm_gain, norm_bias, proj_weight,
         gate_weight, out_gain, out_bias, out_weight):
    tokens = jnp.broadcast_to(token_mask.astype(jnp.float32)[:, None], (token_mask.shape[0], LANES))
    left_k, _, _, _, right_k, state1, gate1, _ = middle_call(
        rows, cols, pieces, parts, pair_state, tokens,
        norm_gain, norm_bias, proj_weight, gate_weight, out_gain, out_bias, out_weight,
    )
    return last_call(left_k, right_k, state1, gate1, out_gain, out_bias, out_weight)


def solution(mesh):
    placed = (P(("groups", "rows"), "cols", None), P("groups"), P(), P(), P(), P(), P(), P(), P())
    rows, cols = mesh.shape["rows"], mesh.shape["cols"]

    def run(pair_state, *rest):
        proj_weight = rest[3]
        channels, hidden = pair_state.shape[2], proj_weight.shape[2] // 4
        extent = pair_state.shape[0]
        fits = channels == hidden == LANES and extent == pair_state.shape[1] and extent <= LANES
        if rows == cols == 4 and fits and extent % (8 * rows) == 0:
            return body(rows, cols, rows, 2 * rows, pair_state, *rest)
        return plain_body(pair_state, *rest)

    return jax.shard_map(
        run,
        mesh=mesh,
        in_specs=placed,
        out_specs=P(("groups", "rows"), "cols", None),
        check_vma=False,
    )
```

time: 671 us -> 573 us (0.85); the launches traced: 671 us -> 566 us
  Pallas kernels: 661 us -> 564 us
    pallas_call x2 -> x1, Pallas kernels: 113 us -> 39.4 us  [last_call(): pl.pallas_call(last_kernel, grid=(LANES // heads,), in_specs=[part, part,...]
    pallas_call x1, Pallas kernels: 548 us -> 525 us  [middle_call(): pl.pallas_call(functools.partial(middle_kernel, rows, cols, n, parts), in...]
where the time goes in v1:
time: 573 us; the launch traced here: 566 us
  Pallas kernels  564 us (98%)
    pallas_call x1, Pallas kernels, middle_call(): pl.pallas_call(functools.partial(middle_kernel, rows, cols, n, parts), in...  525 us
    pallas_call x1, Pallas kernels, last_call(): pl.pallas_call(last_kernel, grid=(LANES // heads,), in_specs=[part, part,...  39.4 us

profile of v1, /device:TPU:1, one launch (start us, length us, event | category | flops | bytes accessed | tf_op | source)
XLA Modules:
  0.0 565.6 jit_solution(5460401505208605471)
XLA Ops:
  0.0 0.7 convert_element_type.3
  0.7 0.8 broadcast_in_dim.2.tokens
  1.5 524.7 %shard_map.91 = (f32[3,4,3072,128]{3,2,1,0:T(8,128)}, f32[4,9216,128]{2,1,0:T(8,128)}, f32[4,9216,128]{2,1,0:T(8,128)}, f32[4,9216,128]{2,1,0:T(8,128)}, f32[3,4...) custom-call(f32[96,96,128]{2,1,0:T(8,128)} %state.1, ...), custom_call_target="tpu_custom_call" | custom-call | tf_op jit(solution)/shard_map/pallas_call | solution.py:728
  526.1 39.4 %shard_map.92 = f32[9216,128]{1,0:T(8,128)} custom-call(f32[3,4,3072,128]{3,2,1,0:T(8,128)} %get-tuple-element.9.left_k, f32[3,4,3072,128]{3,2,1,0:T(8,128)} %get-tuple-element.10.right_k, f32[9216,128]{1,0:T(8,128)} %bitcast.3, f32[9216,128]{1,0:T(8,128)} %bitcast.4, f32[2,128]{1,0:T(2,128)} %out_gain.3, f32[2,128]{1,0:T(2,128)} %out_bias.3, ...), custom_call_target="tpu_custom_call" | custom-call | tf_op jit(solution)/shard_map/pallas_call | solution.py:813

commit v2 on v1

--- a/solution.py
+++ b/solution.py
@@ -136,6 +136,13 @@
     )
 
 
+def across_lanes(x):
+    short = LANES - x.shape[1]
+    if short == 0:
+        return x
+    return jnp.concatenate([x, jnp.zeros((x.shape[0], short), x.dtype)], axis=1)
+
+
 def padded(x):
     rows = x.shape[0]
     if rows == LANES:
@@ -269,8 +276,9 @@
 
         closing(p).start()
         if p:
-            to_across(p).start()
-            to_partner(p).start()
+            if p <= 1:
+                to_across(p).start()
+                to_partner(p).start()
         else:
             for k in range(cuts):
                 for copy in early(k)[1::-1]:
@@ -294,11 +302,11 @@
         def _(g):
             for b in range(4):
                 h = g * 4 + b
-                right = padded(jnp.concatenate(
+                right = jnp.concatenate(
                     [block[pl.ds(pl.multiple_of(o * LANES * m + h * m, 8), m), :] for o in range(rows)], axis=0
-                ))
+                )
                 a3 = jnp.concatenate([high[h], low[h], high[h]], axis=1)
-                turned[half, pl.ds(h, extent, LANES), :] = against(a3, held(right))
+                turned[half, pl.ds(h, extent, LANES), :] = across_lanes(against(a3, held(right)))
 
     def turn(p, q, slot):
         @pl.loop(0, mi)
@@ -562,7 +570,7 @@
         return jnp.logical_and(u >= 0, u < ticks)
 
     order = [(0, p) for p in range(n)] + [(1, p) for p in range(n)]
-    late = 4
+    late = 6
     known = lambda which, p: (p + 1) * parts - 1 + last + max(late + 2, depth)
     turns = ticks + last + max(depth, late, last + 1)
     order.sort(key=lambda step: known(*step))
@@ -587,8 +595,9 @@
                 ending.append(act)
     steps.sort(key=lambda step: step[0])
 
-    half_way = parts // 2
-    some = LANES // (parts - half_way)
+    share_of = 1 << ((parts // 2).bit_length() - 1)
+    half_way = parts - share_of
+    some = LANES // share_of
     for k in range(cuts):
         near_copy, far_copy, on_copy = early(k)
         far_copy.wait_recv()
@@ -621,6 +630,11 @@
         def _():
             turn(p, q, lax.rem(t, 4))
             pass_sums(t, 0)
+
+            @pl.when(jnp.logical_and(q == 0, p + 2 < n))
+            def _():
+                to_across(p + 2).start()
+                to_partner(p + 2).start()
 
             @pl.when(p + 1 < n)
             def _():
@@ -779,10 +793,10 @@
 
     for b in range(heads):
         a = [halves(rows_of(left_k, b, w)) for w in range(wide)]
-        k = [halves(padded(rows_of(right_k, b, w))) for w in range(wide)]
+        k = [halves(rows_of(right_k, b, w)) for w in range(wide)]
         a3 = jnp.concatenate([x[0] for x in a] + [x[1] for x in a] + [x[0] for x in a], axis=1)
         k3 = jnp.concatenate([x[0] for x in k] + [x[0] for x in k] + [x[1] for x in k], axis=1)
-        turned[pl.ds(g * heads + b, extent, LANES), :] = against(a3, k3)
+        turned[pl.ds(g * heads + b, extent, LANES), :] = across_lanes(against(a3, k3))
 
     @pl.when(g == steps - 1)
     def _():
@@ -807,7 +821,7 @@
     wide, n, _, _ = left_k.shape
     size = extent * extent
     f32 = jnp.float32
-    heads = 8
+    heads = 16
     part = pl.BlockSpec((wide, n, heads * (extent // n), LANES), lambda g: (0, 0, g, 0))
     anywhere = pl.BlockSpec(memory_space=pl.ANY)
     out = pl.pallas_call(
@@ -848,7 +862,7 @@
         extent = pair_state.shape[0]
         fits = channels == hidden == LANES and extent == pair_state.shape[1] and extent <= LANES
         if rows == cols == 4 and fits and extent % (8 * rows) == 0:
-            return body(rows, cols, rows, 2 * rows, pair_state, *rest)
+            return body(rows, cols, 6, 8, pair_state, *rest)
         return plain_body(pair_state, *rest)
 
     return jax.shard_map(

time: 573 us -> 541 us (0.944)
  Pallas kernels: 564 us -> 533 us
    pallas_call x1, Pallas kernels: 525 us -> 498 us  [middle_call(): pl.pallas_call(functools.partial(middle_kernel, rows, cols, n, parts), in...]
where the time goes in v2:
time: 541 us; the launch traced here: 535 us
  Pallas kernels  533 us (99%)
    pallas_call x1, Pallas kernels, middle_call(): pl.pallas_call(functools.partial(middle_kernel, rows, cols, n, parts), in...  498 us
    pallas_call x1, Pallas kernels, last_call(): pl.pallas_call(last_kernel, grid=(LANES // heads,), in_specs=[part, part,...  35.4 us

profile of v2, /device:TPU:1, one launch (start us, length us, event | category | flops | bytes accessed | tf_op | source)
XLA Modules:
  0.0 534.9 jit_solution(14951796453424247130)
XLA Ops:
  0.0 0.7 convert_element_type.3
  0.7 0.8 broadcast_in_dim.2.tokens
  1.5 498.1 %shard_map.91 = (f32[3,6,2048,128]{3,2,1,0:T(8,128)}, f32[4,9216,128]{2,1,0:T(8,128)}, f32[4,9216,128]{2,1,0:T(8,128)}, f32[4,9216,128]{2,1,0:T(8,128)}, f32[3,6...) custom-call(f32[96,96,128]{2,1,0:T(8,128)} %state.1, ...), custom_call_target="tpu_custom_call" | custom-call | tf_op jit(solution)/shard_map/pallas_call | solution.py:742
  499.6 35.4 %shard_map.92 = f32[9216,128]{1,0:T(8,128)} custom-call(f32[3,6,2048,128]{3,2,1,0:T(8,128)} %get-tuple-element.9.left_k, f32[3,6,2048,128]{3,2,1,0:T(8,128)} %get-tuple-element.10.right_k, f32[9216,128]{1,0:T(8,128)} %bitcast.3, f32[9216,128]{1,0:T(8,128)} %bitcast.4, f32[2,128]{1,0:T(2,128)} %out_gain.3, f32[2,128]{1,0:T(2,128)} %out_bias.3, ...), custom_call_target="tpu_custom_call" | custom-call | tf_op jit(solution)/shard_map/pallas_call | solution.py:827
